TPU v7x, 32 devices: a 4x4x1 block of a 4x4x8 slice. The times are simulated.
32 devices in a mesh: dp: 1 (over z), cp: 32 (over y, x, core).
Axes of the slice: x: 4, y: 4, z: 1, core: 2. Of those that a mesh axis runs over, the one named last changes fastest.
The devices are a block of a 4x4x8 slice.
Arguments:
- x_in: bfloat16 [16384, 3584], P(('dp', 'cp'))
- dy_in: bfloat16 [16384, 3584], P(('dp', 'cp'))
- doc_id: int32 [16384], P(('dp', 'cp'))
- w_q: bfloat16 [3584, 2, 256], replicated
- w_k: bfloat16 [3584, 1, 256], replicated
- w_v: bfloat16 [3584, 1, 256], replicated
- w_o: bfloat16 [2, 256, 3584], replicated
Outputs:
- output 1: bfloat16 [16384, 3584], P(('dp', 'cp'))
- output 2: bfloat16 [16384, 3584], P(('dp', 'cp'))
All inputs are finite; a program needn't handle non-finite values.
Results may differ from a plain program's by a relative error of at most 0.0092049.
Values are sent between devices in bfloat16 or wider.
A program may use at most 768 MiB of HBM per device.

v0:
```python
import jax
import jax.numpy as jnp
from jax import lax
from jax.sharding import PartitionSpec as P

NEG_BIG = -1.0e30


def stored_positions(seq_len, group_devs):
    tok_dev = seq_len // group_devs
    piece_len = tok_dev // 2
    row_idx = jnp.arange(seq_len, dtype=jnp.int32)
    owner_dev = row_idx // tok_dev
    offset = row_idx % tok_dev
    piece_idx = jnp.where(offset < piece_len, owner_dev, 2 * group_devs - 1 - owner_dev)
    return piece_idx * piece_len + offset % piece_len


def solution(mesh):
    group_devs = mesh.shape['cp']
    row_spec = P(('dp', 'cp'))
    full_spec = P()

    def local_layer(x_in, dy_in, doc_id, w_q, w_k, w_v, w_o):
        tok_dev, d_model = x_in.shape
        q_heads, head_dim = w_q.shape[1], w_q.shape[2]
        kv_heads = w_k.shape[1]
        q_group = q_heads // kv_heads
        seq_len = tok_dev * group_devs
        score_scale = head_dim ** -0.5
        wq_grp = w_q.reshape(d_model, kv_heads, q_group, head_dim)
        wo_grp = w_o.reshape(kv_heads, q_group, head_dim, d_model)
        all_pos = stored_positions(seq_len, group_devs)
        my_pos = lax.dynamic_slice_in_dim(all_pos, lax.axis_index('cp') * tok_dev, tok_dev)
        q_loc = jnp.einsum('td,dkge->tkge', x_in, wq_grp, preferred_element_type=jnp.float32).astype(jnp.bfloat16)
        k_loc = jnp.einsum('td,dke->tke', x_in, w_k, preferred_element_type=jnp.float32).astype(jnp.bfloat16)
        v_loc = jnp.einsum('td,dke->tke', x_in, w_v, preferred_element_type=jnp.float32).astype(jnp.bfloat16)
        k_all = lax.all_gather(k_loc, 'cp', axis=0, tiled=True)
        v_all = lax.all_gather(v_loc, 'cp', axis=0, tiled=True)
        doc_all = lax.all_gather(doc_id, 'cp', axis=0, tiled=True)
        visible = (all_pos[None, :] <= my_pos[:, None]) & (doc_all[None, :] == doc_id[:, None])
        scores = jnp.einsum('tkge,ske->tkgs', q_loc, k_all, preferred_element_type=jnp.float32) * score_scale
        scores = jnp.where(visible[:, None, None, :], scores, NEG_BIG)
        log_norm = jax.nn.logsumexp(scores, axis=-1, keepdims=True)
        prob_bf = jnp.exp(scores - log_norm).astype(jnp.bfloat16)
        out_loc = jnp.einsum('tkgs,ske->tkge', prob_bf, v_all, preferred_element_type=jnp.float32).astype(jnp.bfloat16)
        y_out = jnp.einsum('tkge,kged->td', out_loc, wo_grp, preferred_element_type=jnp.float32).astype(jnp.bfloat16)
        do_loc = jnp.einsum('td,kged->tkge', dy_in, wo_grp, preferred_element_type=jnp.float32).astype(jnp.bfloat16)
        delta_row = jnp.einsum('tkge,tkge->tkg', do_loc, out_loc, preferred_element_type=jnp.float32)
        d_prob = jnp.einsum('tkge,ske->tkgs', do_loc, v_all, preferred_element_type=jnp.float32)
        d_score = (prob_bf.astype(jnp.float32) * (d_prob - delta_row[:, :, :, None])).astype(jnp.bfloat16)
        dq_loc = (jnp.einsum('tkgs,ske->tkge', d_score, k_all, preferred_element_type=jnp.float32) * score_scale).astype(jnp.bfloat16)
        dk_part = jnp.einsum('tkgs,tkge->ske', d_score, q_loc, preferred_element_type=jnp.float32) * score_scale
        dv_part = jnp.einsum('tkgs,tkge->ske', prob_bf, do_loc, preferred_element_type=jnp.float32)
        dk_loc = lax.psum_scatter(dk_part, 'cp', scatter_dimension=0, tiled=True)
        dv_loc = lax.psum_scatter(dv_part, 'cp', scatter_dimension=0, tiled=True)
        dx_wide = (jnp.einsum('tkge,dkge->td', dq_loc, wq_grp, preferred_element_type=jnp.float32)
                   + jnp.einsum('tke,dke->td', dk_loc.astype(jnp.bfloat16), w_k, preferred_element_type=jnp.float32)
                   + jnp.einsum('tke,dke->td', dv_loc.astype(jnp.bfloat16), w_v, preferred_element_type=jnp.float32))
        return y_out, dx_wide.astype(jnp.bfloat16)

    return jax.shard_map(local_layer, mesh=mesh,
                         in_specs=(row_spec, row_spec, row_spec, full_spec, full_spec, full_spec, full_spec),
                         out_specs=(row_spec, row_spec), check_vma=False)
```

profile of v0, /device:TPU:98, one launch (start us, length us, event | category | flops | bytes accessed | tf_op | source)
XLA Modules:
  0.0 462.3 jit_solution(18190632670280011508)
XLA Ops:
  7.3 1.4 copy-done
  8.7 3.8 fusion.64
  12.7 4.4 fusion.61
  17.3 36.1 %all-gather.2 = s32[32,1,512]{2,1,0:T(1,128)S(1)} all-gather(s32[1,1,512]{2,1,0:T(1,128)S(1)} %bitcast.152), channel_id=1, replica_groups=mesh['dp'=1,'cp'=32] {'cp'}, dimensions={0}, use_global_device_ids=true | all-gather | bytes 67584 | tf_op jit(solution)/shard_map/all_gather | solution.py:40
  53.4 6.0 %fusion.48 = bf16[512,2,256]{2,0,1:T(8,128)(2,1)} fusion(bf16[3584,2,256]{2,1,0:T(2,128)(2,1)} %param.10, bf16[512,3584]{1,0:T(8,128)(2,1)} %param.7), kind=kOutput, calls=%fused_computation.44 | convolution fusion | flops 1879310336 | bytes 7864320 | tf_op jit(solution)/shard_map/td,dkge->tkge/dot_general | solution.py:35
  59.4 2.1 fusion.53
  61.5 0.2 copy.39
  61.7 0.1 dynamic_slice.3
  61.8 13.4 %compare_and_fusion = pred[512,16384]{0,1:T(8,128)(4,1)} fusion(s32[512]{0:T(512)S(1)} %copy-done.5, s32[512]{0:T(512)S(1)} %dynamic_slice.3, s32[16384]{0:T(1024)S(1)} %bitcast.151, s32[16384]{0:T(1024)S(1)} %fusion.93), kind=kLoop, calls=%fused_computation.15 | loop fusion | flops 25165824 | bytes 8523776 | tf_op jit(solution)/shard_map/and | solution.py:41
  75.2 29.9 %fusion.1 = (f32[512,2]{0,1:T(2,128)S(1)}, f32[16384,512,2]{1,0,2:T(8,128)}) fusion(pred[512,16384]{0,1:T(8,128)(4,1)} %compare_and_fusion, bf16[512,2,256]{2,0,1:T(8,128)(2,1)} %fusion.48, bf16[16384,256]{1,0:T(8,128)(2,1)} %all-gather.8.cloned.1.call-done), kind=kOutput, calls=%fused_computation.6 | convolution fusion | flops 8640265216 | bytes 84414464 | tf_op jit(solution)/shard_map/tkge,ske->tkgs/dot_general | solution.py:42
  105.1 23.9 %exponential_reduce_fusion = f32[512,2]{0,1:T(2,128)S(1)} fusion(f32[16384,512,2]{1,0,2:T(8,128)} %get-tuple-element.3, f32[512,2]{0,1:T(2,128)S(1)} %is-finite_select_fusion, pred[512,16384]{0,1:T(8,128)(4,1)} %compare_and_fusion), kind=kLoop, calls=%fused_computation.5 | loop fusion | flops 67107840 | bytes 75505664 | tf_op jit(solution)/shard_map/reduce_sum | solution.py:44
  129.0 36.0 %exponential_convert_fusion = bf16[512,1,2,16384]{0,3,2,1:T(8,128)(2,1)} fusion(f32[16384,512,2]{1,0,2:T(8,128)} %get-tuple-element.3, f32[512,2]{0,1:T(2,128)S(1)} %log_add_fusion, pred[512,16384]{0,1:T(8,128)(4,1)} %compare_and_fusion), kind=kLoop, calls=%fused_computation.4 | loop fusion | flops 67108864 | bytes 109056000 | tf_op jit(solution)/shard_map/convert_element_type | solution.py:45
  165.0 17.5 %multiply_reduce_fusion = (f32[512,2]{0,1:T(2,128)S(1)}, bf16[512,2,256]{0,2,1:T(8,128)(2,1)S(1)}) fusion(f32[512,2,256]{0,2,1:T(8,128)S(1)} %copy.39, bf16[512,1,2,16384]{0,3,2,1:T(8,128)(2,1)} %exponential_convert_fusion, bf16[16384,256]{1,0:T(8,128)(2,1)} %all-gather.6.cloned.1.call-done), kind=kOutput, calls=%fused_computation.52 | convolution fusion | flops 8590982144 | bytes 43520000 | tf_op jit(solution)/shard_map/tkgs,ske->tkge/dot_general | solution.py:46
  182.6 25.2 %fusion = bf16[512,1,2,16384]{0,3,2,1:T(8,128)(2,1)} fusion(bf16[512,1,2,16384]{0,3,2,1:T(8,128)(2,1)} %exponential_convert_fusion, bf16[512,2,256]{2,0,1:T(8,128)(2,1)} %copy-done.3, f32[512,2]{0,1:T(2,128)S(1)} %get-tuple-element.4, bf16[16384,256]{1,0:T(8,128)(2,1)} %all-gather.6.cloned.1.call-done), kind=kOutput, calls=%fused_computation.2 | convolution fusion | flops 8657043456 | bytes 76025856 | tf_op jit(solution)/shard_map/tkge,ske->tkgs/dot_general | solution.py:50
  207.8 21.2 %fusion.19 = f32[16384,1,256]{0,2,1:T(8,128)} fusion(bf16[512,2,256]{2,0,1:T(8,128)(2,1)S(1)} %copy-done.7, bf16[512,1,2,16384]{0,3,2,1:T(8,128)(2,1)} %fusion), kind=kOutput, calls=%fused_computation.19 | convolution fusion | flops 8594128896 | bytes 50855936 | tf_op jit(solution)/shard_map/tkgs,tkge->ske/dot_general | solution.py:53
  229.1 0.9 copy-done.4
  230.0 21.1 %fusion.10 = f32[16384,1,256]{0,2,1:T(8,128)} fusion(bf16[512,2,256]{2,0,1:T(8,128)(2,1)S(1)} %copy-done.4, bf16[512,1,2,16384]{0,3,2,1:T(8,128)(2,1)} %exponential_convert_fusion), kind=kOutput, calls=%fused_computation.16 | convolution fusion | flops 8589934592 | bytes 50855936 | tf_op jit(solution)/shard_map/tkgs,tkge->ske/dot_general | solution.py:54
  251.2 6.0 %bitcast_convert_fusion = bf16[512,3584]{1,0:T(8,128)(2,1)} fusion(bf16[512,2,256]{0,2,1:T(8,128)(2,1)S(1)} %get-tuple-element.5, bf16[2,256,3584]{2,1,0:T(8,128)(2,1)} %param.13), kind=kOutput, calls=%fused_computation.28 | convolution fusion | flops 1880883200 | bytes 7864320 | tf_op jit(solution)/shard_map/tkge,kged->td/dot_general | solution.py:47
  257.2 17.9 %fusion.77 = bf16[512,2,256]{0,2,1:T(8,128)(2,1)S(1)} fusion(bf16[512,1,2,16384]{0,3,2,1:T(8,128)(2,1)} %fusion, bf16[16384,256]{1,0:T(8,128)(2,1)} %all-gather.8.cloned.1.call-done), kind=kOutput, calls=%fused_computation.51 | convolution fusion | flops 8590458880 | bytes 42467328 | tf_op jit(solution)/shard_map/tkgs,ske->tkge/dot_general | solution.py:52
  275.1 5.1 %fusion.33 = f32[512,3584,1]{1,0,2:T(8,128)} fusion(bf16[512,2,256]{0,2,1:T(8,128)(2,1)S(1)} %fusion.77, bf16[3584,2,256]{2,1,0:T(2,128)(2,1)S(1)} %copy-done.2), kind=kOutput, calls=%fused_computation.33 | convolution fusion | flops 1879048192 | bytes 11534336 | tf_op jit(solution)/shard_map/tkge,dkge->td/dot_general | solution.py:57
  280.2 56.1 %reduce-scatter.3.cloned.1.call-done = f32[512,1,256]{0,2,1:T(8,128)} async-done(((f32[16384,1,256]{0,2,1:T(8,128)}), f32[512,1,256]{0,2,1:T(8,128)}) %reduce-scatter.3.cloned.1.call-update) | async-done | bytes 524304 | tf_op jit(solution)/shard_map/reduce_scatter | solution.py:55
  336.3 5.2 %fusion.36 = f32[512,3584]{1,0:T(8,128)} fusion(bf16[3584,1,256]{2,0,1:T(8,128)(2,1)S(1)} %copy-done, f32[512,1,256]{0,2,1:T(8,128)} %reduce-scatter.3.cloned.1.call-done), kind=kOutput, calls=%fused_computation.36 | convolution fusion | flops 939655168 | bytes 9699328 | tf_op jit(solution)/shard_map/tke,dke->td/dot_general | solution.py:58
  341.5 105.3 %reduce-scatter.5.cloned.1.call-done = f32[512,1,256]{0,2,1:T(8,128)} async-done(((f32[16384,1,256]{0,2,1:T(8,128)}), f32[512,1,256]{0,2,1:T(8,128)}) %reduce-scatter.5.cloned.1.call-update) | async-done | bytes 524304 | tf_op jit(solution)/shard_map/reduce_scatter | solution.py:56
  446.8 8.9 %fusion.28 = bf16[512,3584]{1,0:T(8,128)(2,1)} fusion(f32[512,3584]{1,0:T(8,128)} %fusion.36, f32[512,3584,1]{1,0,2:T(8,128)} %fusion.33, bf16[3584,1,256]{2,0,1:T(8,128)(2,1)} %param.12, f32[512,1,256]{0,2,1:T(8,128)} %reduce-scatter.5.cloned.1.call-done), kind=kOutput, calls=%fused_computation.27 | convolution fusion | flops 945160192 | bytes 20709376 | tf_op jit(solution)/shard_map/tke,dke->td/dot_general | solution.py:59
  (27 shorter events, 0.6 us)
Async XLA Ops:
  7.2 1.5 copy-start
  7.2 10.1 %copy-start.5 = (s32[512]{0:T(512)S(1)}, s32[512]{0:T(512)}, u32[]{:S(2)}) copy-start(s32[512]{0:T(512)} %param.9) | copy-start | bytes 6148
  7.2 68.0 %all-gather.8.cloned.1.call-start = ((), (), s32[]{:S(2)}) async-start(), calls=%async_computation.5 | async-start | bytes 8650752 | tf_op jit(solution)/shard_map/all_gather | solution.py:38
  12.6 152.4 %all-gather.6.cloned.1.call-start = ((), (), s32[]{:S(2)}) async-start(), calls=%async_computation.4 | async-start | bytes 8650752 | tf_op jit(solution)/shard_map/all_gather | solution.py:39
  17.2 319.2 %reduce-scatter.3.cloned.1.call-start = ((), (), s32[]{:S(2)}) async-start(), calls=%async_computation.2 | async-start | bytes 17301504 | tf_op jit(solution)/shard_map/reduce_scatter | solution.py:55
  17.3 42.1 %copy-start.1 = (bf16[2,256,3584]{2,1,0:T(8,128)(2,1)S(1)}, bf16[2,256,3584]{2,1,0:T(8,128)(2,1)}, u32[]{:S(2)}) copy-start(bf16[2,256,3584]{2,1,0:T(8,128)(2,1)} %param.13) | copy-start | bytes 11010052
  17.3 42.1 %copy-start.6 = (bf16[512,3584]{1,0:T(8,128)(2,1)S(1)}, bf16[512,3584]{1,0:T(8,128)(2,1)}, u32[]{:S(2)}) copy-start(bf16[512,3584]{1,0:T(8,128)(2,1)} %param.8) | copy-start | bytes 11010052
  61.5 43.6 %copy-start.3 = (bf16[512,2,256]{2,0,1:T(8,128)(2,1)}, bf16[512,2,256]{2,0,1:T(8,128)(2,1)S(1)}, u32[]{:S(2)}) copy-start(bf16[512,2,256]{2,0,1:T(8,128)(2,1)S(1)} %fusion.53) | copy-start | bytes 1572868
  182.5 25.2 %copy-start.7 = (bf16[512,2,256]{2,0,1:T(8,128)(2,1)S(1)}, bf16[512,2,256]{2,0,1:T(8,128)(2,1)}, u32[]{:S(2)}) copy-start(bf16[512,2,256]{2,0,1:T(8,128)(2,1)} %fusion.48) | copy-start | bytes 1572868
  229.0 1.0 copy-start.4
  229.0 217.8 %reduce-scatter.5.cloned.1.call-start = ((), (), s32[]{:S(2)}) async-start(), calls=%async_computation.3 | async-start | bytes 17301504 | tf_op jit(solution)/shard_map/reduce_scatter | solution.py:56
  257.2 17.9 %copy-start.2 = (bf16[3584,2,256]{2,1,0:T(2,128)(2,1)S(1)}, bf16[3584,2,256]{2,1,0:T(2,128)(2,1)}, u32[]{:S(2)}) copy-start(bf16[3584,2,256]{2,1,0:T(2,128)(2,1)} %param.10) | copy-start | bytes 11010052
Sparse Core Ops, SparseCore 0:
  12.7 50.5 all-gather.7
  65.4 46.8 all-gather.5
  229.2 107.1 reduce-scatter.2
  339.9 106.8 reduce-scatter.4
where the time goes:
time: 463 us; the launch traced here: 462 us
  matrix products  174 us (38%)
  waiting for transfers between devices  162 us (35%)
  other arithmetic  73.4 us (16%)
  blocking collectives  36.1 us (8%)
  between operations  13.9 us (3%)
    reduce_scatter x1, waiting for transfers between devices, local_layer(): dv_loc = lax.psum_scatter(dv_part, 'cp', scatter_dimension=0, tiled=True)  105 us
    reduce_scatter x1, waiting for transfers between devices, local_layer(): dk_loc = lax.psum_scatter(dk_part, 'cp', scatter_dimension=0, tiled=True)  56.1 us
    all_gather x1, blocking collectives, local_layer(): doc_all = lax.all_gather(doc_id, 'cp', axis=0, tiled=True)  36.1 us
    convert_element_type x1, other arithmetic, local_layer(): prob_bf = jnp.exp(scores - log_norm).astype(jnp.bfloat16)  36 us
    dot_general x1, matrix products, local_layer(): jnp.einsum('tkge,ske->tkgs', q_loc, k_all, preferred_element_type=jnp.flo...  29.9 us
    dot_general x1, matrix products, local_layer(): jnp.einsum('tkge,ske->tkgs', do_loc, v_all, preferred_element_type=jnp.fl...  25.2 us
    reduce_sum x1, other arithmetic, local_layer(): log_norm = jax.nn.logsumexp(scores, axis=-1, keepdims=True)  23.9 us
    dot_general x1, matrix products, local_layer(): jnp.einsum('tkgs,tkge->ske', d_score, q_loc, preferred_element_type=jnp.f...  21.2 us
  transfers between devices with their start and end apart: 4, of which 2 were waited for; matrix products, arithmetic and copies ran while one was open for 37% of the time, Pallas kernels for 0%

commit v1 on v0

v1 whole, which is shorter than its diff:
```python
import functools
import math

import jax
import jax.numpy as jnp
from jax import lax
from jax.experimental import pallas as pl
from jax.experimental.pallas import tpu as pltpu
from jax.sharding import PartitionSpec as P

NEG_BIG = -1.0e30
MESH = pl.DeviceIdType.MESH
VMEM = pltpu.VMEM
F32 = jnp.float32
BF16 = jnp.bfloat16


def remote(src, dst, send_sem, recv_sem, dev):
    return pltpu.make_async_remote_copy(src_ref=src, dst_ref=dst, send_sem=send_sem, recv_sem=recv_sem,
                                        device_id={'cp': dev}, device_id_type=MESH)


def small_gather_kernel(n, x_ref, out_ref, send_sem, recv_sem, own_sem):
    me = lax.axis_index('cp')
    barrier = pltpu.get_barrier_semaphore()

    def greet(off, _):
        pl.semaphore_signal(barrier, inc=1, device_id={'cp': lax.rem(me + off, n)}, device_id_type=MESH)
        return 0
    lax.fori_loop(1, n, greet, 0)
    own = pltpu.make_async_copy(x_ref, out_ref.at[me], own_sem)
    own.start()
    pl.semaphore_wait(barrier, n - 1)

    def send(off, _):
        remote(x_ref, out_ref.at[me], send_sem.at[off], recv_sem.at[off], lax.rem(me + off, n)).start()
        return 0
    lax.fori_loop(1, n, send, 0)
    own.wait()

    def settle(off, _):
        src = lax.rem(me + n - off, n)
        copy = remote(x_ref, out_ref.at[src], send_sem.at[off], recv_sem.at[off], lax.rem(me + off, n))
        copy.wait_send()
        copy.wait_recv()
        return 0
    lax.fori_loop(1, n, settle, 0)


def small_gather(x, n, cid):
    return pl.pallas_call(
        functools.partial(small_gather_kernel, n),
        out_shape=jax.ShapeDtypeStruct((n,) + x.shape, x.dtype),
        in_specs=[pl.BlockSpec(memory_space=VMEM)],
        out_specs=pl.BlockSpec(memory_space=VMEM),
        scratch_shapes=[pltpu.SemaphoreType.DMA((n,)), pltpu.SemaphoreType.DMA((n,)), pltpu.SemaphoreType.DMA],
        compiler_params=pltpu.CompilerParams(collective_id=cid, has_side_effects=True),
        name=f'small_gather_{cid}',
    )(x)


def torus_gather_kernel(side, x_ref, out_ref, send_sem, recv_sem, chip_send, chip_recv, own_sem):
    me = lax.axis_index('cp')
    core = lax.rem(me, 2)
    chip = me // 2
    cx, cy = lax.rem(chip, side), chip // side

    def dev(y, x, c=None):
        y = lax.rem(cy + y + side, side)
        x = lax.rem(cx + x + side, side)
        return (y * side + x) * 2 + (core if c is None else c)

    partner = dev(0, 0, 1 - core)
    barrier = pltpu.get_barrier_semaphore()
    for peer in (dev(0, 1), dev(0, -1), dev(1, 0), dev(-1, 0), partner):
        pl.semaphore_signal(barrier, inc=1, device_id={'cp': peer}, device_id_type=MESH)
    own = pltpu.make_async_copy(x_ref, out_ref.at[me], own_sem)
    own.start()
    pl.semaphore_wait(barrier, 5)

    sends = []

    def at(half, minor, major):
        return dev(major, minor) if half == 0 else dev(minor, major)

    def step(half, axis, amount):
        first = half == axis
        del first
        return at(half, amount, 0) if axis == 0 else at(half, 0, amount)

    slots = [0]
    plan = {}

    def slot(key):
        if key not in plan:
            plan[key] = len(plan)
        return plan[key]

    def ref_of(ref, d, half, ud):
        return ref.at[d, half] if ud is None else ref.at[d, half, ud]

    def send(half, axis, direction, minor, major, ud, own_block):
        d = at(half, minor, major)
        key = slot((half, axis, direction, minor, major, ud))
        src = (x_ref.at[half] if ud is None else x_ref.at[half, ud]) if own_block else ref_of(out_ref, d, half, ud)
        copy = remote(src, ref_of(out_ref, d, half, ud), send_sem.at[key], recv_sem.at[key], step(half, axis, direction))
        copy.start()
        sends.append(copy)

    def receive(half, axis, direction, minor, major, ud):
        key = slot((half, axis, direction, minor, major, ud))
        if axis == 0:
            my_minor, my_major = minor - direction, major
        else:
            my_minor, my_major = minor, major - direction
        d = at(half, my_minor, my_major)
        ref = ref_of(out_ref, d, half, ud)
        remote(ref, ref, send_sem.at[key], recv_sem.at[key], step(half, axis, direction)).wait_recv()
        return my_minor, my_major

    chip_count = [0]
    chip_waits = []

    def to_partner(half, minor, major, ud, own_block=False):
        d = at(half, minor, major)
        k = chip_count[0]
        chip_count[0] += 1
        src = (x_ref.at[half]) if own_block else ref_of(out_ref, d, half, ud)
        copy = remote(src, ref_of(out_ref, d, half, ud), chip_send.at[k], chip_recv.at[k], partner)
        copy.start()
        sends.append(copy)
        chip_waits.append((half, minor, major, ud, k))

    for half in (0, 1):
        for direction in (1, -1):
            send(half, 0, direction, 0, 0, None, True)
    for half in (0, 1):
        for direction in (1, -1):
            send(half, 1, direction, 0, 0, None, True)
        to_partner(half, 0, 0, None, True)

    for direction in (1, -1):
        for half in (0, 1):
            minor, major = receive(half, 0, direction, 0, 0, None)
            ud = 0 if direction == 1 else 1
            send(half, 0, direction, minor, major, ud, False)
            for way in (1, -1):
                send(half, 1, way, minor, major, None, False)
            to_partner(half, minor, major, None)
    for direction in (1, -1):
        for half in (0, 1):
            ud = 0 if direction == 1 else 1
            minor, major = receive(half, 0, direction, -direction, 0, ud)
            for way in (1, -1):
                send(half, 1, way, minor, major, ud, False)
            to_partner(half, minor, major, ud)
    for minor in (0, -1, 1):
        for direction in (1, -1):
            for half in (0, 1):
                _, major = receive(half, 1, direction, minor, 0, None)
                ud = 0 if direction == 1 else 1
                send(half, 1, direction, minor, major, ud, False)
                to_partner(half, minor, major, None)
    for ud, minor in ((0, -2), (1, 2)):
        for direction in (1, -1):
            for half in (0, 1):
                _, major = receive(half, 1, direction, minor, 0, ud)
                if ud == (0 if direction == 1 else 1):
                    send(half, 1, direction, minor, major, ud, False)
                to_partner(half, minor, major, ud)
    for minor in (0, -1, 1):
        for direction in (1, -1):
            for half in (0, 1):
                ud = 0 if direction == 1 else 1
                _, major = receive(half, 1, direction, minor, -direction, ud)
                to_partner(half, minor, major, ud)
    for ud, minor in ((0, -2), (1, 2)):
        for half in (0, 1):
            direction = 1 if ud == 0 else -1
            _, major = receive(half, 1, direction, minor, -direction, ud)
            to_partner(half, minor, major, ud)
    for half, minor, major, ud, k in chip_waits:
        base = at(half, minor, major)
        d = base + 1 - 2 * core
        ref = ref_of(out_ref, d, half, ud)
        remote(ref, ref, chip_send.at[k], chip_recv.at[k], partner).wait_recv()
    for copy in sends:
        copy.wait_send()
    own.wait()


def torus_gather(x, n, cid):
    side = math.isqrt(n // 2)
    return pl.pallas_call(
        functools.partial(torus_gather_kernel, side),
        out_shape=jax.ShapeDtypeStruct((n,) + x.shape, x.dtype),
        in_specs=[pl.BlockSpec(memory_space=VMEM)],
        out_specs=pl.BlockSpec(memory_space=pltpu.HBM),
        scratch_shapes=[pltpu.SemaphoreType.DMA((64,)), pltpu.SemaphoreType.DMA((64,)),
                        pltpu.SemaphoreType.DMA((64,)), pltpu.SemaphoreType.DMA((64,)), pltpu.SemaphoreType.DMA],
        compiler_params=pltpu.CompilerParams(collective_id=cid, has_side_effects=True),
        name='torus_gather',
    )(x)


def dot_nt(a, b):
    return lax.dot_general(a, b, (((1,), (1,)), ((), ())), preferred_element_type=F32)


def dot_nn(a, b):
    return lax.dot_general(a, b, (((1,), (0,)), ((), ())), preferred_element_type=F32)


def query_kernel(pieces, plen, hd, scale, meta, a_ref, start_ref, g_ref, o_ref, dq_ref, ld_ref, kv, p_s, q2, do2, sem):
    half_rows = plen // 2
    for t in range(2):
        c, lo = meta[t], meta[2 + t]
        count = c - lo + 1

        def fetch(i):
            p = lo + i
            far = (p >= pieces // 2).astype(jnp.int32)
            d = jnp.where(far == 1, pieces - 1 - p, p)
            return [pltpu.make_async_copy(g_ref.at[d, h, far, :, pl.ds(0, 2 * hd)], kv.at[i, pl.ds(h * half_rows, half_rows)],
                                          sem.at[h, i]) for h in range(2)]

        def issue(i, _):
            for copy in fetch(i):
                copy.start()
            return 0
        lax.fori_loop(0, count, issue, 0)
        for h in range(2):
            for part in range(2):
                rows = pl.ds(h * plen + part * half_rows, half_rows)
                q2[rows, :] = a_ref[part, t, :, pl.ds((2 + h) * hd, hd)]
                do2[rows, :] = a_ref[part, t, :, pl.ds((4 + h) * hd, hd)]
        first = start_ref[t]
        first = jnp.concatenate([first, first], axis=0)
        row = lax.broadcasted_iota(jnp.int32, (plen, 1), 0) + c * plen
        row = jnp.concatenate([row, row], axis=0)

        def scores(i):
            s = dot_nt(q2[...], kv[i, :, pl.ds(0, hd)]) * scale
            col = lax.broadcasted_iota(jnp.int32, (1, plen), 1) + (lo + i) * plen
            return jnp.where((col >= first) & (col <= row), s, NEG_BIG)

        def sweep_norm(i, carry):
            m, l = carry
            for copy in fetch(i):
                copy.wait()
            s = scores(i)
            parts = [s[:, k:k + 128] for k in range(0, plen, 128)]
            m_new = m
            for part in parts:
                m_new = jnp.maximum(m_new, part)
            l = l * jnp.exp(m - m_new)
            for part in parts:
                l = l + jnp.exp(part - m_new)
            return m_new, l
        m, l = lax.fori_loop(0, count, sweep_norm,
                             (jnp.full((2 * plen, 128), NEG_BIG, F32), jnp.zeros((2 * plen, 128), F32)))
        top = jnp.max(m, axis=1, keepdims=True)
        total = jnp.sum(l * jnp.exp(m - top), axis=1, keepdims=True)
        log_norm = top + jnp.log(total)

        def sweep_out(i, acc):
            p = jnp.exp(scores(i) - log_norm).astype(BF16)
            p_s[i] = p
            return acc + dot_nn(p, kv[i, :, pl.ds(hd, hd)])
        out = lax.fori_loop(0, count, sweep_out, jnp.zeros((2 * plen, hd), F32)).astype(BF16)
        delta = jnp.sum(do2[...].astype(F32) * out.astype(F32), axis=1, keepdims=True)

        def sweep_dq(i, acc):
            dp = dot_nt(do2[...], kv[i, :, pl.ds(hd, hd)])
            ds = (p_s[i].astype(F32) * (dp - delta)).astype(BF16)
            return acc + dot_nn(ds, kv[i, :, pl.ds(0, hd)])
        dq = (lax.fori_loop(0, count, sweep_dq, jnp.zeros((2 * plen, hd), F32)) * scale).astype(BF16)
        for h in range(2):
            o_ref[pl.ds(t * plen, plen), pl.ds(h * hd, hd)] = out[h * plen:(h + 1) * plen]
            dq_ref[pl.ds(t * plen, plen), pl.ds(h * hd, hd)] = dq[h * plen:(h + 1) * plen]
        lrow = jnp.transpose(jnp.broadcast_to(log_norm, (2 * plen, 128)))
        drow = jnp.transpose(jnp.broadcast_to(delta, (2 * plen, 128)))
        for h in range(2):
            ld_ref[pl.ds(4 * t + h, 1), :] = lrow[0:1, h * plen:(h + 1) * plen]
            ld_ref[pl.ds(4 * t + 2 + h, 1), :] = drow[0:1, h * plen:(h + 1) * plen]


def key_kernel(pieces, plen, hd, scale, meta, a_ref, end_ref, ld_ref, g_ref, dk_ref, dv_ref, qd, kt, vt, dk_acc, dv_acc, sem):
    half_rows = plen // 2
    for t in range(2):
        c, hi = meta[t], meta[4 + t]
        count = hi - c + 1

        def fetch(i):
            p = c + i
            far = (p >= pieces // 2).astype(jnp.int32)
            d = jnp.where(far == 1, pieces - 1 - p, p)
            b = lax.rem(i, 2)
            return [pltpu.make_async_copy(g_ref.at[d, h, far, :, pl.ds(2 * hd, 4 * hd)],
                                          qd.at[b, pl.ds(h * half_rows, half_rows)], sem.at[b, h]) for h in range(2)]

        for copy in fetch(0):
            copy.start()
        for part in range(2):
            rows = pl.ds(part * half_rows, half_rows)
            kt[rows, :] = a_ref[part, t, :, pl.ds(0, hd)]
            vt[rows, :] = a_ref[part, t, :, pl.ds(hd, hd)]
        dk_acc[...] = jnp.zeros_like(dk_acc)
        dv_acc[...] = jnp.zeros_like(dv_acc)
        last = end_ref[t]
        key = lax.broadcasted_iota(jnp.int32, (plen, 1), 0) + c * plen

        def sweep(i, _):
            @pl.when(i + 1 < count)
            def _():
                for copy in fetch(i + 1):
                    copy.start()
            for copy in fetch(i):
                copy.wait()
            b = lax.rem(i, 2)
            p_idx = c + i
            far = (p_idx >= pieces // 2).astype(jnp.int32)
            d = jnp.where(far == 1, pieces - 1 - p_idx, p_idx)
            col = lax.broadcasted_iota(jnp.int32, (1, plen), 1) + p_idx * plen
            seen = (col >= key) & (col <= last)
            for h in range(2):
                qh = qd[b, :, pl.ds(h * hd, hd)]
                doh = qd[b, :, pl.ds((2 + h) * hd, hd)]
                st = dot_nt(kt[...], qh) * scale
                st = jnp.where(seen, st, NEG_BIG)
                norm = ld_ref[d, pl.ds(4 * far + h, 1), :]
                delta = ld_ref[d, pl.ds(4 * far + 2 + h, 1), :]
                pt = jnp.exp(st - norm).astype(BF16)
                dv_acc[...] += dot_nn(pt, doh)
                dpt = dot_nt(vt[...], doh)
                dst = (pt.astype(F32) * (dpt - delta)).astype(BF16)
                dk_acc[...] += dot_nn(dst, qh)
            return 0
        lax.fori_loop(0, count, sweep, 0)
        dk_ref[pl.ds(t * plen, plen), :] = (dk_acc[...] * scale).astype(BF16)
        dv_ref[pl.ds(t * plen, plen), :] = dv_acc[...].astype(BF16)


def solution(mesh):
    n = mesh.shape['cp']
    row_spec = P(('dp', 'cp'))
    full_spec = P()

    def local_layer(x_in, dy_in, doc_id, w_q, w_k, w_v, w_o):
        tok, d_model = x_in.shape
        heads, hd = w_q.shape[1], w_q.shape[2]
        plen = tok // 2
        pieces = 2 * n
        seq = tok * n
        scale = hd ** -0.5
        me = lax.axis_index('cp')
        wq = w_q.reshape(d_model, heads * hd)
        wk = w_k.reshape(d_model, hd)
        wv = w_v.reshape(d_model, hd)
        wo = w_o.reshape(heads * hd, d_model)

        lane = 128
        doc_pad = jnp.zeros((8, lane), jnp.int32).at[:tok // lane].set(doc_id.reshape(tok // lane, lane))
        docs = small_gather(doc_pad, n, 1)[:, :tok // lane].reshape(n, 2, plen)
        doc_all = jnp.concatenate([docs[:, 0].reshape(-1), docs[::-1, 1].reshape(-1)])
        start = jnp.sum((doc_all[None, :] < doc_id[:, None]).astype(jnp.int32), axis=1)
        end = jnp.sum((doc_all[None, :] <= doc_id[:, None]).astype(jnp.int32), axis=1) - 1
        own = jnp.stack([me, pieces - 1 - me]).astype(jnp.int32)
        meta = jnp.concatenate([own, start[::plen] // plen, end[plen - 1::plen] // plen]).astype(jnp.int32)

        def mm(a, b):
            return jnp.dot(a, b, preferred_element_type=F32).astype(BF16)
        k_loc, v_loc, q_loc = mm(x_in, wk), mm(x_in, wv), mm(x_in, wq)
        do_loc = lax.dot_general(dy_in, wo, (((1,), (1,)), ((), ())), preferred_element_type=F32).astype(BF16)
        a_loc = jnp.concatenate([k_loc, v_loc, q_loc, do_loc], axis=1)
        width = a_loc.shape[1]
        a_loc = a_loc.reshape(2, 2, plen // 2, width).transpose(1, 0, 2, 3)
        g_all = torus_gather(a_loc, n, 2)

        smem = pl.BlockSpec(memory_space=pltpu.SMEM)
        vmem = pl.BlockSpec(memory_space=VMEM)
        hbm = pl.BlockSpec(memory_space=pltpu.HBM)
        o_loc, dq_loc, ld = pl.pallas_call(
            functools.partial(query_kernel, pieces, plen, hd, scale),
            out_shape=(jax.ShapeDtypeStruct((tok, heads * hd), BF16), jax.ShapeDtypeStruct((tok, heads * hd), BF16),
                       jax.ShapeDtypeStruct((8, plen), F32)),
            in_specs=[smem, vmem, vmem, hbm], out_specs=(vmem, vmem, vmem),
            scratch_shapes=[VMEM((pieces, plen, 2 * hd), BF16), VMEM((pieces, 2 * plen, plen), BF16),
                            VMEM((2 * plen, hd), BF16), VMEM((2 * plen, hd), BF16), pltpu.SemaphoreType.DMA((2, pieces))],
            compiler_params=pltpu.CompilerParams(vmem_limit_bytes=60 * 1024 * 1024),
            name='query_side',
        )(meta, a_loc, start.reshape(2, plen, 1), g_all)
        ld_all = small_gather(ld, n, 3)
        dk_loc, dv_loc = pl.pallas_call(
            functools.partial(key_kernel, pieces, plen, hd, scale),
            out_shape=(jax.ShapeDtypeStruct((tok, hd), BF16), jax.ShapeDtypeStruct((tok, hd), BF16)),
            in_specs=[smem, vmem, vmem, vmem, hbm], out_specs=(vmem, vmem),
            scratch_shapes=[VMEM((2, plen, 4 * hd), BF16), VMEM((plen, hd), BF16), VMEM((plen, hd), BF16),
                            VMEM((plen, hd), F32), VMEM((plen, hd), F32), pltpu.SemaphoreType.DMA((2, 2))],
            name='key_side',
        )(meta, a_loc, end.reshape(2, plen, 1), ld_all, g_all)
        y_out = mm(o_loc, wo)
        nt = (((1,), (1,)), ((), ()))
        dx = (lax.dot_general(dq_loc, wq, nt, preferred_element_type=F32)
              + lax.dot_general(dk_loc, wk, nt, preferred_element_type=F32)
              + lax.dot_general(dv_loc, wv, nt, preferred_element_type=F32))
        return y_out, dx.astype(BF16)

    return jax.shard_map(local_layer, mesh=mesh,
                         in_specs=(row_spec, row_spec, row_spec, full_spec, full_spec, full_spec, full_spec),
                         out_specs=(row_spec, row_spec), check_vma=False)
```

time: 463 us -> 257 us (0.56)
  Pallas kernels: 0 us -> 211 us
  waiting for transfers between devices: 162 us -> 0 us
  matrix products: 174 us -> 21.2 us
  other arithmetic: 73.4 us -> 8.44 us
  blocking collectives: 36.1 us -> 0 us
  between operations: 13.9 us -> 0.88 us
  local copies, waits for them, and re-layouts: 2.65 us -> 12.2 us
    pallas_call x0 -> x5, Pallas kernels: none -> 211 us  [the longest x1 137 us: torus_gather(): pl.pallas_call(functools.partial(torus_gather_kernel, side), out_shape=ja...]
    reduce_scatter x2 -> x0, waiting for transfers between devices: 161 us -> none  [the longest x1 105 us: local_layer(): dv_loc = lax.psum_scatter(dv_part, 'cp', scatter_dimension=0, tiled=True)]
    dot_general x14 -> x8, matrix products: 174 us -> 21.2 us  [the longest x4 12.9 us: mm(): return jnp.dot(a, b, preferred_element_type=F32).astype(BF16)]
    all_gather x1 -> x0, blocking collectives: 36.1 us -> none  [local_layer(): doc_all = lax.all_gather(doc_id, 'cp', axis=0, tiled=True)]
    convert_element_type x1 -> x0, other arithmetic: 36 us -> none  [local_layer(): prob_bf = jnp.exp(scores - log_norm).astype(jnp.bfloat16)]
    reduce_sum x1, other arithmetic: 23.9 us -> 7.71 us  [local_layer(): jnp.sum((doc_all[None, :] < doc_id[:, None]).astype(jnp.int32), axis=1)]
    and x1 -> x0, other arithmetic: 13.4 us -> none  [local_layer(): (all_pos[None, :] <= my_pos[:, None]) & (doc_all[None, :] == doc_id[:, No...]
  transfers between devices with their start and end apart: 4 -> 0, of which waited for: 2 -> 0; matrix products, arithmetic and copies ran while one was open for 37% -> 0% of each run, Pallas kernels for 0% -> 0%
where the time goes in v1:
time: 257 us; the launch traced here: 254 us
  Pallas kernels  211 us (82%)
  matrix products  21.2 us (8%)
  local copies, waits for them, and re-layouts  12.2 us (5%)
  other arithmetic  8.44 us (3%)
    pallas_call x1, Pallas kernels, torus_gather(): pl.pallas_call(functools.partial(torus_gather_kernel, side), out_shape=ja...  137 us
    pallas_call x2, Pallas kernels, small_gather(): pl.pallas_call(functools.partial(small_gather_kernel, n), out_shape=jax.S...  47.4 us
    pallas_call x1, Pallas kernels, local_layer(): pl.pallas_call(functools.partial(query_kernel, pieces, plen, hd, scale),...  13.8 us
    dot_general x4, matrix products, mm(): return jnp.dot(a, b, preferred_element_type=F32).astype(BF16)  12.9 us
    pallas_call x1, Pallas kernels, local_layer(): pl.pallas_call(functools.partial(key_kernel, pieces, plen, hd, scale), ou...  12.6 us
    reduce_sum x1, other arithmetic, local_layer(): jnp.sum((doc_all[None, :] < doc_id[:, None]).astype(jnp.int32), axis=1)  7.71 us

profile of v1, /device:TPU:98, one launch (start us, length us, event | category | flops | bytes accessed | tf_op | source)
XLA Modules:
  0.0 253.9 jit_solution(15138796799644270531)
XLA Ops:
  0.6 1.4 scatter.4.x_ref
  2.1 12.8 %small_gather_1.1 = s32[32,8,128]{2,1,0:T(8,128)} custom-call(s32[8,128]{1,0:T(8,128)} %scatter.4.x_ref), custom_call_target="tpu_custom_call" | custom-call | tf_op jit(solution)/shard_map/small_gather_1/pallas_call | solution.py:51
  14.9 0.9 slice.31
  16.0 7.7 %convert_reduce_fusion.1 = (s32[512]{0:T(512)S(1)}, s32[512]{0:T(512)S(1)}) fusion(s32[16384]{0:T(1024)S(1)} %pad_add_fusion, s32[512]{0:T(512)} %param.11), kind=kLoop, calls=%fused_computation.1 | loop fusion | flops 50330624 | bytes 71680 | tf_op jit(solution)/shard_map/reduce_sum | solution.py:366
  23.9 0.6 pad_add_fusion.1.meta
  24.5 0.9 reshape.77.start_ref
  25.4 0.9 sub.21.end_ref
  26.4 3.3 %fusion.7 = bf16[512,256]{0,1:T(8,128)(2,1)S(1)} fusion(bf16[512,3584]{1,0:T(8,128)(2,1)} %param.9, bf16[3584,1,256]{2,0,1:T(8,128)(2,1)S(1)} %copy-done), kind=kOutput, calls=%fused_computation.15 | convolution fusion | flops 939655168 | bytes 5767168 | tf_op jit(solution)/shard_map/dot_general | solution.py:372
  30.1 1.2 fusion.10
  31.2 0.9 copy-done.9
  32.1 1.1 copy-done.11
  33.2 2.1 convolution_convert_fusion.1
  35.3 0.8 copy.17
  36.2 2.3 convolution_convert_fusion.2
  38.6 1.6 copy.13
  40.2 2.6 %copy.19 = bf16[2,2,128,1536]{3,2,0,1:T(8,128)(2,1)} copy(bf16[2,2,128,1536]{3,2,1,0:T(8,128)(2,1)} %bitcast.43) | data formatting | bytes 3145728 | tf_op jit(solution)/shard_map/reshape | solution.py:377
  42.8 137.3 %torus_gather.1.g_ref = bf16[32,2,2,128,1536]{4,3,2,1,0:T(8,128)(2,1)} custom-call(bf16[2,2,128,1536]{3,2,1,0:T(8,128)(2,1)} %bitcast.38), custom_call_target="tpu_custom_call" | custom-call | tf_op jit(solution)/shard_map/torus_gather/pallas_call | solution.py:194
  180.2 13.8 %query_side.1 = (bf16[512,512]{1,0:T(8,128)(2,1)}, bf16[512,512]{1,0:T(8,128)(2,1)}, f32[8,256]{1,0:T(8,128)}) custom-call(s32[6]{0:T(128)} %pad_add_fusion.1.meta, bf16[2,2,128,1536]{3,2,1,0:T(8,128)(2,1)} %bitcast.39, s32[2,256,1]{2,1,0:T(8,128)} %reshape.77.start_ref, bf16[32,2,2,128,1536]{4,3,2,1,0:T(8,128)(2,1)} %torus_gather.1.g_ref), custom_call_target="tpu_custom_call" | custom-call | tf_op jit(solution)/shard_map/query_side/pallas_call | solution.py:383
  194.0 34.6 %small_gather_3.1.ld_ref = f32[32,8,256]{2,1,0:T(8,128)} custom-call(f32[8,256]{1,0:T(8,128)} %get-tuple-element.21.x_ref), custom_call_target="tpu_custom_call" | custom-call | tf_op jit(solution)/shard_map/small_gather_3/pallas_call | solution.py:51
  228.6 12.6 %key_side.1 = (bf16[512,256]{1,0:T(8,128)(2,1)}, bf16[512,256]{1,0:T(8,128)(2,1)}) custom-call(s32[6]{0:T(128)} %pad_add_fusion.1.meta, bf16[2,2,128,1536]{3,2,1,0:T(8,128)(2,1)} %bitcast.40, s32[2,256,1]{2,1,0:T(8,128)} %sub.21.end_ref, f32[32,8,256]{2,1,0:T(8,128)} %small_gather_3.1.ld_ref, bf16[32,2,2,128,1536]{4,3,2,1,0:T(8,128)(2,1)} %torus_gather.1.g_ref), custom_call_target="tpu_custom_call" | custom-call | tf_op jit(solution)/shard_map/key_side/pallas_call | solution.py:394
  241.2 6.1 %convolution_convert_fusion = bf16[512,3584]{1,0:T(8,128)(2,1)} fusion(bf16[512,512]{1,0:T(8,128)(2,1)S(1)} %copy-done.12, bf16[512,3584]{1,0:T(8,128)(2,1)} %bitcast.48), kind=kOutput, calls=%fused_computation.3 | convolution fusion | flops 1880883200 | bytes 7864320 | tf_op jit(solution)/shard_map/dot_general | solution.py:372
  247.3 2.1 fusion.14
  249.5 1.1 fusion.3
  250.9 3.0 %add_convert_fusion = bf16[512,3584]{1,0:T(8,128)(2,1)} fusion(f32[512,3584]{1,0:T(8,128)S(1)} %fusion.14, f32[512,3584]{1,0:T(8,128)S(1)} %fusion.3, bf16[512,256]{1,0:T(8,128)(2,1)S(1)} %copy-done.7, bf16[3584,1,256]{2,0,1:T(8,128)(2,1)S(1)} %copy-done.5), kind=kOutput, calls=%fused_computation.2 | convolution fusion | flops 945029120 | bytes 20447232 | tf_op jit(solution)/shard_map/dot_general | solution.py:406
  (33 shorter events, 1.2 us)
Async XLA Ops:
  0.6 25.7 %copy-start = (bf16[3584,1,256]{2,0,1:T(8,128)(2,1)S(1)}, bf16[3584,1,256]{2,0,1:T(8,128)(2,1)}, u32[]{:S(2)}) copy-start(bf16[3584,1,256]{2,0,1:T(8,128)(2,1)} %param.13) | copy-start | bytes 5505028
  26.3 3.4 %copy-start.4 = (bf16[3584,1,256]{2,0,1:T(8,128)(2,1)S(1)}, bf16[3584,1,256]{2,0,1:T(8,128)(2,1)}, u32[]{:S(2)}) copy-start(bf16[3584,1,256]{2,0,1:T(8,128)(2,1)} %param.14) | copy-start | bytes 5505028
  26.4 3.7 %copy-start.10 = (bf16[512,3584]{1,0:T(8,128)(2,1)S(1)}, bf16[512,3584]{1,0:T(8,128)(2,1)}, u32[]{:S(2)}) copy-start(bf16[512,3584]{1,0:T(8,128)(2,1)} %param.9) | copy-start | bytes 11010052
  30.0 2.0 copy-start.9
  30.0 3.2 %copy-start.11 = (bf16[2,256,3584]{2,1,0:T(8,128)(2,1)S(1)}, bf16[2,256,3584]{2,1,0:T(8,128)(2,1)}, u32[]{:S(2)}) copy-start(bf16[2,256,3584]{2,1,0:T(8,128)(2,1)} %param.15) | copy-start | bytes 11010052
  33.2 2.1 copy-start.3
  36.1 2.3 copy-start.1
  228.6 12.6 %copy-start.12 = (bf16[512,512]{1,0:T(8,128)(2,1)S(1)}, bf16[512,512]{1,0:T(8,128)(2,1)}, u32[]{:S(2)}) copy-start(bf16[512,512]{1,0:T(8,128)(2,1)} %get-tuple-element.19) | copy-start | bytes 1572868
  241.2 6.1 %copy-start.2 = (bf16[448,8,2,256]{3,1,2,0:T(8,128)(2,1)S(1)}, bf16[448,8,2,256]{3,1,2,0:T(8,128)(2,1)}, u32[]{:S(2)}) copy-start(bf16[448,8,2,256]{3,1,2,0:T(8,128)(2,1)} %copy-done.1) | copy-start | bytes 11010052
  241.2 6.1 %copy-start.6 = (bf16[512,512]{1,0:T(8,128)(2,1)S(1)}, bf16[512,512]{1,0:T(8,128)(2,1)}, u32[]{:S(2)}) copy-start(bf16[512,512]{1,0:T(8,128)(2,1)} %get-tuple-element.20) | copy-start | bytes 1572868
  247.3 2.1 copy-start.8
  249.4 1.5 copy-start.5
  249.5 1.5 copy-start.7
